TPU v7x, 32 devices: a whole 2x2x4 slice. The times are simulated.
32 devices in a mesh: node: 4 (over y, x), torus: 8 (over z, core).
Axes of the slice: x: 2, y: 2, z: 4, core: 2. Of those that a mesh axis runs over, the one named last changes fastest.
Arguments:
- tokens: bfloat16 [4096, 7168], P(('node', 'torus')), may hold values from -6 to 6
- expert_ids: int32 [4096, 8], P(('node', 'torus')), may hold values from 0 to 383, as said below
- route_weight: bfloat16 [4096, 8], P(('node', 'torus')), may hold values from 0.19921875 to 2.5
- w_gate: bfloat16 [16, 7168, 1024], P('torus', None, 'node'), may hold values from -0.0625 to 0.0625
- w_up: bfloat16 [16, 7168, 1024], P('torus', None, 'node'), may hold values from -0.0625 to 0.0625
- w_down: bfloat16 [16, 1024, 7168], P('torus', 'node'), may hold values from -0.1875 to 0.1875
Outputs:
- moe_out: bfloat16 [4096, 7168], P(('node', 'torus'))
Inputs may be any that keep to these rules, and one draw needn't show every extreme that they name: `expert_ids`: each row names 8 different experts. Counting an expert e below 16 as one of group e // 2, at most 4 of the 128 rows of one device (aligned blocks of rows, in order) name an expert of any one group, and in every draw some group is named by exactly 4 rows of every device.
All inputs are finite; a program needn't handle non-finite values.
Results may differ from a plain program's by a relative error of at most 0.0095.
Values may be sent and summed in bfloat16 or wider, within the bound.
A program may use at most 128 MiB of HBM per device.

v0:
```python
import functools

import jax
import jax.numpy as jnp
from jax import lax
from jax.experimental import pallas as pl
from jax.experimental.pallas import tpu as pltpu
from jax.sharding import PartitionSpec as P

CAP = 4
QBLOCK = 128
PARTS = 4
SUB = CAP * PARTS
CHUNK = 1024
WIDE = CHUNK // PARTS
MESH = pl.DeviceIdType.MESH
F32 = jnp.float32
BF16 = jnp.bfloat16


def flipped(index, mask):
    value = index
    bit = 0
    while mask >> bit:
        if (mask >> bit) & 1:
            size = 1 << bit
            value = value + size * (1 - 2 * lax.rem(lax.div(index, jnp.int32(size)), jnp.int32(2)))
        bit += 1
    return value


def dot(left, right):
    return jnp.dot(left, right, preferred_element_type=F32)


def kernel(
    groups, chunks, lags,
    tok_hbm, ids_ref, rw_ref, wg_hbm, wu_hbm, wd_hbm, out_hbm,
    tok, wg, wu, wd, place, place_t, perm, perm_t,
    sent, held, wsent, wheld, xs, acc, hidden, wcol,
    part, relay_a, relay_b, got_x, got_y, back_s, back, obuf,
    sems, lsems,
):
    node = lax.axis_index("node")
    torus = lax.axis_index("torus")
    rows = tok.shape[0]
    subs = groups * SUB
    slots = groups * CAP
    half = slots // 2
    shalf = subs // 2
    units = subs // 128
    experts = wg.shape[0]
    at_x = (flipped(node, 1), torus)
    at_y = (flipped(node, 2), torus)
    at_z = [(node, flipped(torus, j)) for j in range(groups)]

    tok_cp, wg_cp, wu_cp, wd_cp = [], [], [], []
    for k in range(chunks):
        cols = pl.ds(k * CHUNK, CHUNK)
        tok_cp.append(pltpu.make_async_copy(tok_hbm.at[:, cols], tok.at[:, cols], lsems.at[0, k]))
        wg_cp.append(pltpu.make_async_copy(wg_hbm.at[:, cols, :], wg.at[:, cols, :], lsems.at[1, k]))
        wu_cp.append(pltpu.make_async_copy(wu_hbm.at[:, cols, :], wu.at[:, cols, :], lsems.at[2, k]))
        wd_cp.append(pltpu.make_async_copy(wd_hbm.at[:, :, cols], wd.at[:, :, cols], lsems.at[3, k]))
    for c in tok_cp:
        c.start()
    for a, b in zip(wg_cp, wu_cp):
        a.start()
        b.start()
    for c in wd_cp:
        c.start()

    barrier = pltpu.get_barrier_semaphore()
    for peer in at_z[1:] + [at_x, at_y]:
        pl.semaphore_signal(barrier, inc=1, device_id=peer, device_id_type=MESH)

    row = lax.broadcasted_iota(jnp.int32, (subs, rows), 0)
    gid = jnp.bitwise_xor(row // SUB, jnp.full((subs, rows), torus, jnp.int32))
    slot_of = (row // PARTS) % CAP
    part_of = row % PARTS
    hit = jnp.zeros((subs, rows), F32)
    chosen = [jnp.zeros((subs, rows), F32) for _ in range(experts)]
    weights = rw_ref[...].astype(F32)
    for k in range(ids_ref.shape[0]):
        named = jnp.broadcast_to(ids_ref[k : k + 1, :], (subs, rows))
        weight = jnp.broadcast_to(weights[k : k + 1, :], (subs, rows))
        for e in range(experts):
            same = named == gid * experts + e
            hit = jnp.where(same, 1.0, hit)
            chosen[e] = jnp.where(same, weight, chosen[e])
    lower = lax.broadcasted_iota(jnp.int32, (rows, rows), 0) < lax.broadcasted_iota(
        jnp.int32, (rows, rows), 1
    )
    before = dot(hit.astype(BF16), lower.astype(F32).astype(BF16))
    onehot = jnp.where(before == slot_of.astype(F32), hit, 0.0)
    lane = lax.broadcasted_iota(jnp.int32, (subs, 128), 1)
    wrow = jnp.zeros((subs, 128), F32)
    for e in range(experts):
        total = jnp.sum(onehot * chosen[e], axis=1, keepdims=True)
        wrow = jnp.where(lane == e, total, wrow)
    wsent[...] = wrow.astype(BF16)
    wheld[0, 0:SUB] = wrow[0:SUB].astype(BF16)
    for q in range(PARTS):
        place[q] = jnp.where(part_of == q, onehot, 0.0).astype(BF16)
    pr = lax.broadcasted_iota(jnp.int32, (128, 128), 0)
    pc = lax.broadcasted_iota(jnp.int32, (128, 128), 1)
    ur = 128 // PARTS
    perm[...] = (pc == (pr % ur) * PARTS + pr // ur).astype(F32).astype(BF16)
    perm_t[...] = (pr == (pc % ur) * PARTS + pc // ur).astype(F32).astype(BF16)

    pl.semaphore_wait(barrier, groups + 1)

    def remote(src, dst, a, b, k, peer):
        copy = pltpu.make_async_remote_copy(
            src_ref=src, dst_ref=dst, send_sem=sems.at[a, k], recv_sem=sems.at[b, k],
            device_id=peer, device_id_type=MESH,
        )
        copy.start()

    def wait(ref, a, k):
        pltpu.make_async_copy(ref, ref, sems.at[a, k]).wait()

    def views(k):
        if k == chunks:
            return wsent, wheld
        return sent.at[k], held.at[k]

    def exchange(k):
        src, dst = views(k)
        for j in range(1, groups):
            at = pl.ds(j * SUB, SUB)
            remote(src.at[at], dst.at[0, at], 0, 1, k, at_z[j])

    def spread(k):
        _, dst = views(k)
        wait(dst.at[0, pl.ds(SUB, subs - SUB)], 1, k)
        remote(dst.at[0], dst.at[1], 2, 3, k, at_x)
        remote(dst.at[0], dst.at[2], 4, 5, k, at_y)

    def forward(k):
        _, dst = views(k)
        wait(dst.at[1], 3, k)
        remote(dst.at[1, pl.ds(0, shalf)], dst.at[3, pl.ds(0, shalf)], 6, 7, k, at_y)
        wait(dst.at[2], 5, k)
        remote(dst.at[2, pl.ds(shalf, shalf)], dst.at[3, pl.ds(shalf, shalf)], 8, 9, k, at_x)

    def arrived(k):
        _, dst = views(k)
        wait(dst.at[3, pl.ds(0, shalf)], 7, k)
        wait(dst.at[3, pl.ds(shalf, shalf)], 9, k)

    def make(k):
        tok_cp[k].wait()
        picked = jnp.zeros((subs, WIDE), F32)
        for q in range(PARTS):
            picked += dot(place[q], tok[:, k * CHUNK + q * WIDE : k * CHUNK + (q + 1) * WIDE])
        for b in range(WIDE // QBLOCK):
            block = picked[:, b * QBLOCK : (b + 1) * QBLOCK]
            largest = jnp.max(jnp.abs(block), axis=1, keepdims=True)
            scale = ((largest + 1e-06) * (1.0 / 448.0)).astype(BF16).astype(F32)
            coded = (block / scale).astype(BF16).astype(F32)
            value = (coded * scale).astype(BF16)
            sent[k, :, b * QBLOCK : (b + 1) * QBLOCK] = value
            held[k, 0, 0:SUB, b * QBLOCK : (b + 1) * QBLOCK] = value[0:SUB]

    def unit_rows(r, u):
        return r * slots + u * ur

    def multiply(k):
        for r in range(4):
            for u in range(units):
                moved = dot(perm[...], held[k, r, u * 128 : (u + 1) * 128, :]).astype(BF16)
                at = unit_rows(r, u)
                for q in range(PARTS):
                    xs[at : at + ur, q * WIDE : (q + 1) * WIDE] = moved[q * ur : (q + 1) * ur]
        wg_cp[k].wait()
        wu_cp[k].wait()
        cols = pl.ds(k * CHUNK, CHUNK)
        for e in range(experts):
            for s, w in enumerate((wg, wu)):
                got = dot(xs[...], w[e, cols, :])
                if k == 0:
                    acc[e, s] = got
                else:
                    acc[e, s] += got

    exchange(chunks)
    l2, l3, l4 = lags
    flip_at = min(chunks, l4) - 1
    for step in range(chunks + l4):
        if step < chunks:
            make(step)
            exchange(step)
        if step == flip_at:
            for q in range(PARTS):
                place_t[q] = place[q].astype(F32).T.astype(BF16)
        if step == l2:
            spread(chunks)
        if 0 <= step - l2 < chunks:
            spread(step - l2)
        if step == l3:
            forward(chunks)
        if 0 <= step - l3 < chunks:
            forward(step - l3)
        if step == l4:
            arrived(chunks)
            for r in range(4):
                for u in range(units):
                    moved = dot(perm[...], wheld[r, u * 128 : (u + 1) * 128, :])
                    at = unit_rows(r, u)
                    wcol[at : at + ur, :] = moved[0:ur]
        if 0 <= step - l4 < chunks:
            arrived(step - l4)
            multiply(step - l4)

    for e in range(experts):
        gate = acc[e, 0]
        hidden[e] = (gate / (1.0 + jnp.exp(-gate)) * acc[e, 1]).astype(BF16)

    def down(k):
        wd_cp[k].wait()
        for r in range(4):
            at = pl.ds(r * slots, slots)
            total = jnp.zeros((slots, CHUNK), F32)
            for e in range(experts):
                got = dot(hidden[e, at, :], wd[e, :, k * CHUNK : (k + 1) * CHUNK])
                total += wcol[at, e : e + 1] * got
            part[k, r] = total.astype(BF16)
        remote(part.at[k, 3, pl.ds(0, half)], relay_a.at[k], 10, 11, k, at_y)
        remote(part.at[k, 3, pl.ds(half, half)], relay_b.at[k], 12, 13, k, at_x)

    def merge(k):
        wait(relay_a.at[k], 11, k)
        part[k, 1, 0:half] = (part[k, 1, 0:half].astype(F32) + relay_a[k].astype(F32)).astype(BF16)
        remote(part.at[k, 1], got_x.at[k], 14, 15, k, at_x)
        wait(relay_b.at[k], 13, k)
        part[k, 2, half:slots] = (
            part[k, 2, half:slots].astype(F32) + relay_b[k].astype(F32)
        ).astype(BF16)
        remote(part.at[k, 2], got_y.at[k], 16, 17, k, at_y)

    def home(k):
        wait(got_x.at[k], 15, k)
        wait(got_y.at[k], 17, k)
        for u in range(units):
            at = pl.ds(u * ur, ur)
            total = (
                part[k, 0, at].astype(F32) + got_x[k, at].astype(F32) + got_y[k, at].astype(F32)
            ).astype(BF16)
            stacked = jnp.concatenate(
                [total[:, q * WIDE : (q + 1) * WIDE] for q in range(PARTS)], axis=0
            )
            moved = dot(perm_t[...], stacked).astype(BF16)
            back_s[k, u * 128 : (u + 1) * 128] = moved
            if u == 0:
                back[k, 0:SUB] = moved[0:SUB]
        for j in range(1, groups):
            at = pl.ds(j * SUB, SUB)
            remote(back_s.at[k, at], back.at[k, at], 18, 19, k, at_z[j])

    out_cp = [
        pltpu.make_async_copy(obuf.at[k], out_hbm.at[:, pl.ds(k * CHUNK, CHUNK)], lsems.at[4, k])
        for k in range(chunks)
    ]

    def finish(k):
        wait(back.at[k, pl.ds(SUB, subs - SUB)], 19, k)
        for q in range(PARTS):
            obuf[k, :, q * WIDE : (q + 1) * WIDE] = dot(place_t[q], back[k]).astype(BF16)
        out_cp[k].start()

    for step in range(chunks + l4):
        if step < chunks:
            down(step)
        if 0 <= step - l2 < chunks:
            merge(step - l2)
        if 0 <= step - l3 < chunks:
            home(step - l3)
        if 0 <= step - l4 < chunks:
            finish(step - l4)

    for k in range(chunks + 1):
        src, dst = views(k)
        wait(src.at[pl.ds(SUB, subs - SUB)], 0, k)
        wait(dst.at[0], 2, k)
        wait(dst.at[0], 4, k)
        wait(dst.at[1, pl.ds(0, shalf)], 6, k)
        wait(dst.at[2, pl.ds(shalf, shalf)], 8, k)
    for k in range(chunks):
        wait(relay_a.at[k], 10, k)
        wait(relay_b.at[k], 12, k)
        wait(got_x.at[k], 14, k)
        wait(got_y.at[k], 16, k)
        wait(back_s.at[k, pl.ds(SUB, subs - SUB)], 18, k)
        out_cp[k].wait()


LAGS = (3, 6, 9)


def shards(tokens, expert_ids, route_weight, w_gate, w_up, w_down):
    groups = lax.axis_size("torus")
    rows, width = tokens.shape
    experts, _, units = w_gate.shape
    chunks = width // CHUNK
    subs = groups * SUB
    slots = groups * CAP
    anywhere = pl.BlockSpec(memory_space=pl.ANY)
    local = pl.BlockSpec(memory_space=pltpu.VMEM)
    V = pltpu.VMEM
    return pl.pallas_call(
        functools.partial(kernel, groups, chunks, LAGS),
        out_shape=jax.ShapeDtypeStruct((rows, width), BF16),
        in_specs=[anywhere, local, local, anywhere, anywhere, anywhere],
        out_specs=anywhere,
        scratch_shapes=[
            V((rows, width), BF16),
            V(w_gate.shape, BF16),
            V(w_up.shape, BF16),
            V(w_down.shape, BF16),
            V((PARTS, subs, rows), BF16),
            V((PARTS, rows, subs), BF16),
            V((128, 128), BF16),
            V((128, 128), BF16),
            V((chunks, subs, WIDE), BF16),
            V((chunks, 4, subs, WIDE), BF16),
            V((subs, 128), BF16),
            V((4, subs, 128), BF16),
            V((4 * slots, CHUNK), BF16),
            V((experts, 2, 4 * slots, units), F32),
            V((experts, 4 * slots, units), BF16),
            V((4 * slots, 128), F32),
            V((chunks, 4, slots, CHUNK), BF16),
            V((chunks, slots // 2, CHUNK), BF16),
            V((chunks, slots // 2, CHUNK), BF16),
            V((chunks, slots, CHUNK), BF16),
            V((chunks, slots, CHUNK), BF16),
            V((chunks, subs, WIDE), BF16),
            V((chunks, subs, WIDE), BF16),
            V((chunks, rows, CHUNK), BF16),
            pltpu.SemaphoreType.DMA((20, chunks + 1)),
            pltpu.SemaphoreType.DMA((5, chunks)),
        ],
        compiler_params=pltpu.CompilerParams(
            collective_id=0, has_side_effects=True, vmem_limit_bytes=64000000
        ),
    )(tokens, expert_ids.T, route_weight.T, w_gate, w_up, w_down)


def solution(mesh):
    placed = (
        P(("node", "torus"), None),
        P(("node", "torus"), None),
        P(("node", "torus"), None),
        P("torus", None, "node"),
        P("torus", None, "node"),
        P("torus", "node", None),
    )
    return jax.shard_map(
        shards, mesh=mesh, in_specs=placed, out_specs=P(("node", "torus"), None), check_vma=False
    )
```

profile of v0, /device:TPU:0, one launch (start us, length us, event | category | flops | bytes accessed | tf_op | source)
XLA Modules:
  0.0 57.4 jit_solution(9811306025872023418)
XLA Ops:
  0.0 54.5 %shard_map.64 = bf16[128,7168]{1,0:T(8,128)(2,1)} custom-call(bf16[128,7168]{1,0:T(8,128)(2,1)} %tok_hbm.1, s32[8,128]{1,0:T(8,128)} %bitcast.2, bf16[8,128]{1,0:T(8,128)(2,1)} %bitcast.3, bf16[2,7168,256]{2,1,0:T(8,128)(2,1)} %wg_hbm.1, bf16[2,7168,256]{2,1,0:T(8,128)(2,1)} %wu_hbm.1, bf16[2,256,7168]{2,1,0:T(8,128)(2,1)} %wd_hbm.1), custom_call_target="tpu_custom_call" | custom-call | tf_op jit(solution)/shard_map/pallas_call | solution.py:310
  54.5 2.8 %copy.8 = bf16[128,7168]{1,0:T(8,128)(2,1)} copy(bf16[128,7168]{1,0:T(8,128)(2,1)} %shard_map.64) | data formatting | bytes 3670016
where the time goes:
time: 57.6 us; the launch traced here: 57.4 us
  Pallas kernels  54.5 us (95%)
  local copies, waits for them, and re-layouts  2.85 us (5%)
    pallas_call x1, Pallas kernels, shards(): pl.pallas_call(functools.partial(kernel, groups, chunks, LAGS), out_shape...  54.5 us
    unnamed x1, local copies, waits for them, and re-layouts  2.85 us

commit v1 on v0

v1 whole, which is shorter than its diff:
```python
import functools

import jax
import jax.numpy as jnp
from jax import lax
from jax.experimental import pallas as pl
from jax.experimental.pallas import tpu as pltpu
from jax.sharding import PartitionSpec as P

CAP = 4
QBLOCK = 128
PARTS = 4
SUB = CAP * PARTS
CHUNK = 1024
WIDE = CHUNK // PARTS
MESH = pl.DeviceIdType.MESH
F32 = jnp.float32
BF16 = jnp.bfloat16

KINDS = (
    "z1", "z2", "z3", "x0", "x1", "x2", "x3", "y0", "y1", "y2", "y3",
    "fy0", "fy2", "fy3", "fx1", "fx2", "fx3",
    "ra0", "rb0", "gx0", "gy0", "zr0", "ra1", "rb1", "gx1", "gy1", "zr1",
    "wz", "wx", "wy", "wf",
)

TIMES = {
    "make": (0.0, 0.4),
    "late": (2.7, 0.01),
    "spread1": (1.75, 0.4),
    "forward0": (3.3, 0.45),
    "spread3": (4.4, 0.75),
    "forward1": (5.0, 0.5),
    "wspread": (6.0, 0.0),
    "forward3": (8.0, 1.0),
    "wforward": (9.0, 0.0),
    "spread2": (9.2, 0.6),
    "multiply1": (10.7, 1.0),
    "forward2": (12.2, 0.5),
    "warrived": (13.0, 0.0),
    "multiply0": (17.0, 0.45),
    "down1": (16.9, 0.35),
    "merge1": (19.4, 0.5),
    "home1": (22.0, 0.9),
    "down0": (20.5, 0.4),
    "merge0": (23.0, 0.6),
    "home0": (26.0, 0.95),
    "finish": (29.5, 0.95),
}


def flipped(index, mask):
    value = index
    bit = 0
    while mask >> bit:
        if (mask >> bit) & 1:
            size = 1 << bit
            value = value + size * (1 - 2 * lax.rem(lax.div(index, jnp.int32(size)), jnp.int32(2)))
        bit += 1
    return value


def dot(left, right):
    return jnp.dot(left, right, preferred_element_type=F32)


def kernel(
    groups, chunks,
    tok_hbm, ids_hbm, rw_hbm, wg_hbm, wu_hbm, wd_hbm, out_hbm,
    tok, ids, rw, wg, wu, wd, place, place_t, perm, perm_t,
    sent, held, wsent, warr, whold, xs, acc, hidden, wcol,
    part, relay_a, relay_b, got_x, got_y, back_s, back, obuf,
    ssems, rsems, lsems,
):
    node = lax.axis_index("node")
    torus = lax.axis_index("torus")
    rows = tok.shape[0]
    subs = groups * SUB
    fold = groups // 2
    sh = fold * SUB
    slots = fold * CAP
    lots = 4 * slots
    side = CHUNK // 2
    unit = min(128, sh)
    experts = wg.shape[0]
    peers = [j for j in range(groups) if not j & 2] + [j for j in range(groups) if j & 2]
    at_x = (flipped(node, 1), torus)
    at_y = (flipped(node, 2), torus)
    at_z = [(node, flipped(torus, j)) for j in range(groups)]

    barrier = pltpu.get_barrier_semaphore()
    for peer in at_z[1:] + [at_x, at_y]:
        pl.semaphore_signal(barrier, inc=1, device_id=peer, device_id_type=MESH)

    ids_cp = pltpu.make_async_copy(ids_hbm, ids, lsems.at[5, 0])
    rw_cp = pltpu.make_async_copy(rw_hbm, rw, lsems.at[5, 1])
    ids_cp.start()
    rw_cp.start()
    tok_cp, wg_cp, wu_cp, wd_cp = [], [], [], []
    for k in range(chunks):
        cols = pl.ds(k * CHUNK, CHUNK)
        tok_cp.append(pltpu.make_async_copy(tok_hbm.at[:, cols], tok.at[:, cols], lsems.at[0, k]))
        wg_cp.append(pltpu.make_async_copy(wg_hbm.at[:, cols, :], wg.at[:, cols, :], lsems.at[1, k]))
        wu_cp.append(pltpu.make_async_copy(wu_hbm.at[:, cols, :], wu.at[:, cols, :], lsems.at[2, k]))
        wd_cp.append(pltpu.make_async_copy(wd_hbm.at[:, :, cols], wd.at[:, :, cols], lsems.at[3, k]))
    for c in tok_cp:
        c.start()
    for a, b in zip(wg_cp, wu_cp):
        a.start()
        b.start()
    for c in wd_cp:
        c.start()

    pr = lax.broadcasted_iota(jnp.int32, (128, 128), 0)
    pc = lax.broadcasted_iota(jnp.int32, (128, 128), 1)
    ur = 128 // PARTS
    perm[...] = (pc == (pr % ur) * PARTS + pr // ur).astype(F32).astype(BF16)
    tr = lax.broadcasted_iota(jnp.int32, (unit, unit), 0)
    tc = lax.broadcasted_iota(jnp.int32, (unit, unit), 1)
    tu = unit // PARTS
    perm_t[...] = (tr == (tc % tu) * PARTS + tc // tu).astype(F32).astype(BF16)

    def distance(at):
        inner = at % fold
        return (inner // 2) * 4 + (at // fold) * 2 + inner % 2

    ids_cp.wait()
    rw_cp.wait()
    row = lax.broadcasted_iota(jnp.int32, (subs, rows), 0)
    gid = jnp.bitwise_xor(distance(row // SUB), jnp.full((subs, rows), torus, jnp.int32))
    slot_of = (row // PARTS) % CAP
    part_of = row % PARTS
    hit = jnp.zeros((subs, rows), F32)
    chosen = [jnp.zeros((subs, rows), F32) for _ in range(experts)]
    weights = rw[...].astype(F32)
    for k in range(ids.shape[0]):
        named = jnp.broadcast_to(ids[k : k + 1, :], (subs, rows))
        weight = jnp.broadcast_to(weights[k : k + 1, :], (subs, rows))
        for e in range(experts):
            same = named == gid * experts + e
            hit = jnp.where(same, 1.0, hit)
            chosen[e] = jnp.where(same, weight, chosen[e])
    lower = lax.broadcasted_iota(jnp.int32, (rows, rows), 0) < lax.broadcasted_iota(
        jnp.int32, (rows, rows), 1
    )
    before = dot(hit.astype(BF16), lower.astype(F32).astype(BF16))
    onehot = jnp.where(before == slot_of.astype(F32), hit, 0.0)
    for q in range(PARTS):
        place[q] = jnp.where(part_of == q, onehot, 0.0).astype(BF16)
    lane = lax.broadcasted_iota(jnp.int32, (subs, 128), 1)
    from_j = distance(lax.broadcasted_iota(jnp.int32, (subs, 128), 0) // SUB)
    wrow = jnp.zeros((subs, 128), F32)
    for e in range(experts):
        total = jnp.sum(onehot * chosen[e], axis=1, keepdims=True)
        wrow = jnp.where(lane == from_j * experts + e, total, wrow)
    wsent[...] = wrow.astype(BF16)
    warr[0:SUB] = wrow[0:SUB].astype(BF16)

    pl.semaphore_wait(barrier, groups + 1)

    def remote(kind, k, src, dst, peer):
        at = KINDS.index(kind)
        copy = pltpu.make_async_remote_copy(
            src_ref=src, dst_ref=dst, send_sem=ssems.at[at], recv_sem=rsems.at[at, k],
            device_id=peer, device_id_type=MESH,
        )
        copy.start()

    def wait(kind, k, ref):
        pltpu.make_async_copy(ref, ref, rsems.at[KINDS.index(kind), k]).wait()

    def sent_all(kind, ref):
        pltpu.make_async_copy(ref, ref, ssems.at[KINDS.index(kind)]).wait()

    def lanes(k):
        return pl.ds(k * WIDE, WIDE)

    classes = ((0, 0, 1), (0, 1, 2), (0, 2, fold), (1, 0, fold))

    def rows_of(c, r, k, lo=None, hi=None):
        h, first, last = classes[c]
        lo = first if lo is None else lo
        hi = last if hi is None else hi
        at = pl.ds(r * sh + lo * SUB, (hi - lo) * SUB)
        return held.at[h, at, :] if k is None else held.at[h, at, lanes(k)]

    def halves(c):
        h, lo, hi = classes[c]
        mid = {0: hi, 1: lo}.get(c, (lo + hi) // 2)
        return lo, mid, hi

    def exchange(c, k):
        h, lo, hi = classes[c]
        for p in range(lo, hi):
            at = (h * fold + p) * SUB
            src = sent.at[pl.ds(at, SUB), lanes(k)]
            dst = held.at[h, pl.ds(p * SUB, SUB), lanes(k)]
            remote(f"z{c}", k, src, dst, at_z[peers[h * fold + p]])

    def spread(c, k):
        if c:
            wait(f"z{c}", k, rows_of(c, 0, k))
        remote(f"x{c}", k, rows_of(c, 0, k), rows_of(c, 1, k), at_x)
        remote(f"y{c}", k, rows_of(c, 0, k), rows_of(c, 2, k), at_y)

    def forward(c, k):
        lo, mid, hi = halves(c)
        if mid > lo:
            wait(f"x{c}", k, rows_of(c, 1, k))
            remote(f"fy{c}", k, rows_of(c, 1, k, lo, mid), rows_of(c, 3, k, lo, mid), at_y)
        if hi > mid:
            wait(f"y{c}", k, rows_of(c, 2, k))
            remote(f"fx{c}", k, rows_of(c, 2, k, mid, hi), rows_of(c, 3, k, mid, hi), at_x)

    def arrived(c, k):
        lo, mid, hi = halves(c)
        if mid == hi:
            wait(f"y{c}", k, rows_of(c, 2, k))
        if lo == mid:
            wait(f"x{c}", k, rows_of(c, 1, k))
        if mid > lo:
            wait(f"fy{c}", k, rows_of(c, 3, k, lo, mid))
        if hi > mid:
            wait(f"fx{c}", k, rows_of(c, 3, k, mid, hi))

    def make(k):
        tok_cp[k].wait()
        picked = jnp.zeros((subs, WIDE), F32)
        for q in range(PARTS):
            picked += dot(place[q], tok[:, k * CHUNK + q * WIDE : k * CHUNK + (q + 1) * WIDE])
        for b in range(WIDE // QBLOCK):
            block = picked[:, b * QBLOCK : (b + 1) * QBLOCK]
            largest = jnp.max(jnp.abs(block), axis=1, keepdims=True)
            scale = ((largest + 1e-06) * (1.0 / 448.0)).astype(BF16).astype(F32)
            coded = (block / scale).astype(BF16).astype(F32)
            value = (coded * scale).astype(BF16)
            at = k * WIDE + b * QBLOCK
            sent[:, at : at + QBLOCK] = value
            held[0, 0:SUB, at : at + QBLOCK] = value[0:SUB]
        exchange(3, k)
        exchange(1, k)
        spread(0, k)
        if k == 0:
            for p in range(1, groups):
                at = pl.ds(p * SUB, SUB)
                remote("wz", 0, wsent.at[at], warr.at[at], at_z[peers[p]])

    def wspread(_):
        wait("wz", 0, warr.at[pl.ds(SUB, subs - SUB)])
        total = jnp.zeros((SUB, 128), F32)
        for p in range(groups):
            total += warr[p * SUB : (p + 1) * SUB].astype(F32)
        whold[0:SUB] = total.astype(BF16)
        remote("wx", 0, whold.at[pl.ds(0, SUB)], whold.at[pl.ds(SUB, SUB)], at_x)
        remote("wy", 0, whold.at[pl.ds(0, SUB)], whold.at[pl.ds(2 * SUB, SUB)], at_y)

    def wforward(_):
        wait("wx", 0, whold.at[pl.ds(SUB, SUB)])
        remote("wf", 0, whold.at[pl.ds(SUB, SUB)], whold.at[pl.ds(3 * SUB, SUB)], at_y)

    def warrived(_):
        wait("wy", 0, whold.at[pl.ds(2 * SUB, SUB)])
        wait("wf", 0, whold.at[pl.ds(3 * SUB, SUB)])
        er = lax.broadcasted_iota(jnp.int32, (lots, 4 * SUB), 0)
        ec = lax.broadcasted_iota(jnp.int32, (lots, 4 * SUB), 1)
        pick = ec == (er // slots) * SUB + (er % CAP) * PARTS
        spun = dot(pick.astype(F32).astype(BF16), whold[...])
        wl = lax.broadcasted_iota(jnp.int32, (lots, 128), 1)
        place_in = (lax.broadcasted_iota(jnp.int32, (lots, 128), 0) % slots) // CAP
        for h in range(2):
            far = distance(place_in + h * fold)
            for e in range(experts):
                mine = jnp.where(wl == far * experts + e, spun, 0.0)
                column = jnp.sum(mine, axis=1, keepdims=True)
                wcol[h, e] = jnp.broadcast_to(column, (lots, 128))

    def multiply(h, k):
        for c in range(4):
            if classes[c][0] == h:
                arrived(c, k)
        for u in range(4 * sh // 128):
            moved = dot(perm[...], held[h, u * 128 : (u + 1) * 128, k * WIDE : (k + 1) * WIDE])
            moved = moved.astype(BF16)
            for q in range(PARTS):
                xs[h, u * ur : (u + 1) * ur, q * WIDE : (q + 1) * WIDE] = moved[q * ur : (q + 1) * ur]
        wg_cp[k].wait() if h else None
        wu_cp[k].wait() if h else None
        cols = pl.ds(k * CHUNK, CHUNK)
        for e in range(experts):
            for s, w in enumerate((wg, wu)):
                got = dot(xs[h], w[e, cols, :])
                if k == 0:
                    acc[h, e, s] = got
                else:
                    acc[h, e, s] += got
        if k == chunks - 1:
            for e in range(experts):
                gate = acc[h, e, 0]
                hidden[h, e] = (gate / (1.0 + jnp.exp(-gate)) * acc[h, e, 1]).astype(BF16)

    def down(h, k):
        wd_cp[k].wait() if h else None
        cols = pl.ds(k * CHUNK, CHUNK)
        total = jnp.zeros((lots, CHUNK), F32)
        for e in range(experts):
            got = dot(hidden[h, e], wd[e, :, k * CHUNK : (k + 1) * CHUNK])
            total += jnp.tile(wcol[h, e], (1, CHUNK // 128)) * got
        part[h, :, cols] = total.astype(BF16)
        at = pl.ds(3 * slots, slots)
        low, high = pl.ds(k * CHUNK, side), pl.ds(k * CHUNK + side, side)
        remote(f"ra{h}", k, part.at[h, at, low], relay_a.at[h, :, pl.ds(k * side, side)], at_y)
        remote(f"rb{h}", k, part.at[h, at, high], relay_b.at[h, :, pl.ds(k * side, side)], at_x)

    def merge(h, k):
        cols = pl.ds(k * CHUNK, CHUNK)
        for kind, relay, r, got, lo, peer in (
            ("a", relay_a, 1, got_x, k * CHUNK, at_x), ("b", relay_b, 2, got_y, k * CHUNK + side, at_y),
        ):
            here = pl.ds(k * side, side)
            wait(f"r{kind}{h}", k, relay.at[h, :, here])
            at, where = pl.ds(r * slots, slots), pl.ds(lo, side)
            total = part[h, at, where].astype(F32) + relay[h, :, here].astype(F32)
            part[h, at, where] = total.astype(BF16)
            sort = "gx" if kind == "a" else "gy"
            remote(f"{sort}{h}", k, part.at[h, at, cols], got.at[h, :, cols], peer)

    def home(h, k):
        cols = pl.ds(k * CHUNK, CHUNK)
        wait(f"gx{h}", k, got_x.at[h, :, cols])
        wait(f"gy{h}", k, got_y.at[h, :, cols])
        total = (
            part[h, 0:slots, cols].astype(F32) + got_x[h, :, cols].astype(F32) + got_y[h, :, cols].astype(F32)
        ).astype(BF16)
        for u in range(sh // unit):
            stacked = jnp.concatenate(
                [total[u * tu : (u + 1) * tu, q * WIDE : (q + 1) * WIDE] for q in range(PARTS)], axis=0
            )
            moved = dot(perm_t[...], stacked).astype(BF16)
            at = h * sh + u * unit
            back_s[at : at + unit, k * WIDE : (k + 1) * WIDE] = moved
            if h == 0 and u == 0:
                back[0:SUB, k * WIDE : (k + 1) * WIDE] = moved[0:SUB]
        for p in range(h * fold, (h + 1) * fold):
            if p:
                at = pl.ds(p * SUB, SUB)
                remote(f"zr{h}", k, back_s.at[at, lanes(k)], back.at[at, lanes(k)], at_z[peers[p]])

    out_cp = [
        pltpu.make_async_copy(obuf.at[k], out_hbm.at[:, pl.ds(k * CHUNK, CHUNK)], lsems.at[4, k])
        for k in range(chunks)
    ]

    def finish(k):
        if k == 0:
            for q in range(PARTS):
                place_t[q] = place[q].astype(F32).T.astype(BF16)
        wait("zr1", k, back.at[pl.ds(sh, sh), lanes(k)])
        wait("zr0", k, back.at[pl.ds(SUB, sh - SUB), lanes(k)])
        for q in range(PARTS):
            obuf[k, :, q * WIDE : (q + 1) * WIDE] = dot(
                place_t[q], back[:, k * WIDE : (k + 1) * WIDE]
            ).astype(BF16)
        out_cp[k].start()

    stages = {"make": make, "late": lambda k: exchange(2, k), "finish": finish}
    for c in range(4):
        stages[f"spread{c}"] = functools.partial(spread, c)
        stages[f"forward{c}"] = functools.partial(forward, c)
    for h in range(2):
        for name, stage in (("multiply", multiply), ("down", down), ("merge", merge), ("home", home)):
            stages[f"{name}{h}"] = functools.partial(stage, h)
    once = {"wspread": wspread, "wforward": wforward, "warrived": warrived}
    tasks = []
    for name, (start, step) in TIMES.items():
        for k in range(1 if name in once else chunks):
            tasks.append((start + step * k, name, k))
    for _, name, k in sorted(tasks):
        (once.get(name) or stages[name])(k)

    for c in range(4):
        h, first, last = classes[c]
        lo, mid, hi = halves(c)
        if c:
            sent_all(f"z{c}", sent.at[pl.ds((h * fold + first) * SUB, (last - first) * SUB), :])
        sent_all(f"x{c}", rows_of(c, 0, None))
        sent_all(f"y{c}", rows_of(c, 0, None))
        if mid > lo:
            sent_all(f"fy{c}", rows_of(c, 1, None, lo, mid))
        if hi > mid:
            sent_all(f"fx{c}", rows_of(c, 2, None, mid, hi))
    sent_all("wz", wsent.at[pl.ds(SUB, subs - SUB)])
    for kind in ("wx", "wy", "wf"):
        sent_all(kind, whold.at[pl.ds(0, SUB)])
    for h in range(2):
        sent_all(f"ra{h}", relay_a.at[h])
        sent_all(f"rb{h}", relay_b.at[h])
        sent_all(f"gx{h}", got_x.at[h])
        sent_all(f"gy{h}", got_y.at[h])
        at = pl.ds(h * sh + (0 if h else SUB), sh - (0 if h else SUB))
        sent_all(f"zr{h}", back_s.at[at, :])
    for c in out_cp:
        c.wait()


def shards(tokens, expert_ids, route_weight, w_gate, w_up, w_down):
    groups = lax.axis_size("torus")
    rows, width = tokens.shape
    experts, _, units = w_gate.shape
    chunks = width // CHUNK
    subs = groups * SUB
    fold = groups // 2
    sh = fold * SUB
    slots = fold * CAP
    lots = 4 * slots
    span = chunks * WIDE
    anywhere = pl.BlockSpec(memory_space=pl.ANY)
    V = pltpu.VMEM
    return pl.pallas_call(
        functools.partial(kernel, groups, chunks),
        out_shape=jax.ShapeDtypeStruct((rows, width), BF16),
        in_specs=[anywhere] * 6,
        out_specs=anywhere,
        scratch_shapes=[
            V((rows, width), BF16),
            V((expert_ids.shape[1], rows), jnp.int32),
            V((expert_ids.shape[1], rows), BF16),
            V(w_gate.shape, BF16),
            V(w_up.shape, BF16),
            V(w_down.shape, BF16),
            V((PARTS, subs, rows), BF16),
            V((PARTS, rows, subs), BF16),
            V((128, 128), BF16),
            V((min(128, sh), min(128, sh)), BF16),
            V((subs, span), BF16),
            V((2, 4 * sh, span), BF16),
            V((subs, 128), BF16),
            V((subs, 128), BF16),
            V((4 * SUB, 128), BF16),
            V((2, lots, CHUNK), BF16),
            V((2, experts, 2, lots, units), F32),
            V((2, experts, lots, units), BF16),
            V((2, experts, lots, 128), F32),
            V((2, lots, width), BF16),
            V((2, slots, width // 2), BF16),
            V((2, slots, width // 2), BF16),
            V((2, slots, width), BF16),
            V((2, slots, width), BF16),
            V((subs, span), BF16),
            V((subs, span), BF16),
            V((chunks, rows, CHUNK), BF16),
            pltpu.SemaphoreType.DMA((len(KINDS),)),
            pltpu.SemaphoreType.DMA((len(KINDS), chunks)),
            pltpu.SemaphoreType.DMA((6, chunks)),
        ],
        compiler_params=pltpu.CompilerParams(
            collective_id=0, has_side_effects=True, vmem_limit_bytes=64000000
        ),
    )(tokens, expert_ids.T, route_weight.T, w_gate, w_up, w_down)


def solution(mesh):
    placed = (
        P(("node", "torus"), None),
        P(("node", "torus"), None),
        P(("node", "torus"), None),
        P("torus", None, "node"),
        P("torus", None, "node"),
        P("torus", "node", None),
    )
    return jax.shard_map(
        shards, mesh=mesh, in_specs=placed, out_specs=P(("node", "torus"), None), check_vma=False
    )
```

time: 57.6 us -> 56 us (0.972)
  Pallas kernels: 54.5 us -> 53 us
    pallas_call x1, Pallas kernels: 54.5 us -> 53 us  [shards(): pl.pallas_call(functools.partial(kernel, groups, chunks), out_shape=jax.S...]
where the time goes in v1:
time: 56 us; the launch traced here: 55.9 us
  Pallas kernels  53 us (95%)
  local copies, waits for them, and re-layouts  2.85 us (5%)
    pallas_call x1, Pallas kernels, shards(): pl.pallas_call(functools.partial(kernel, groups, chunks), out_shape=jax.S...  53 us
    unnamed x1, local copies, waits for them, and re-layouts  2.85 us

profile of v1, /device:TPU:0, one launch (start us, length us, event | category | flops | bytes accessed | tf_op | source)
XLA Modules:
  0.0 55.9 jit_solution(7271032060552200431)
XLA Ops:
  0.0 53.0 %shard_map.64 = bf16[128,7168]{1,0:T(8,128)(2,1)} custom-call(bf16[128,7168]{1,0:T(8,128)(2,1)} %tok_hbm.1, s32[8,128]{1,0:T(8,128)} %bitcast.2, bf16[8,128]{1,0:T(8,128)(2,1)} %bitcast.3, bf16[2,7168,256]{2,1,0:T(8,128)(2,1)} %wg_hbm.1, bf16[2,7168,256]{2,1,0:T(8,128)(2,1)} %wu_hbm.1, bf16[2,256,7168]{2,1,0:T(8,128)(2,1)} %wd_hbm.1), custom_call_target="tpu_custom_call" | custom-call | tf_op jit(solution)/shard_map/pallas_call | solution.py:418
  53.0 2.8 %copy.8 = bf16[128,7168]{1,0:T(8,128)(2,1)} copy(bf16[128,7168]{1,0:T(8,128)(2,1)} %shard_map.64) | data formatting | bytes 3670016

commit v2 on v1

v2 whole, which is shorter than its diff:
```python
import functools

import jax
import jax.numpy as jnp
from jax import lax
from jax.experimental import pallas as pl
from jax.experimental.pallas import tpu as pltpu
from jax.sharding import PartitionSpec as P

CAP = 4
QBLOCK = 128
PARTS = 4
SUB = CAP * PARTS
CHUNK = 1024
WIDE = CHUNK // PARTS
MESH = pl.DeviceIdType.MESH
F32 = jnp.float32
BF16 = jnp.bfloat16

KINDS = ("z1", "z2", "z3", "t0", "t1", "t2", "t3", "a0", "a1", "r0", "r1", "g0", "g1", "zr")
EARLY = 4

PLACES = {
    "make": (0, 1, 2, 4, 5, 6, 9),
    "spread1": (3, 7, 8, 11, 12, 15, 57),
    "forward0": (10, 13, 49, 52, 54, 55, 65),
    "late": (14, 17, 19, 21, 23, 35, 38),
    "spread3": (16, 22, 24, 25, 26, 28, 30),
    "wspread": (18,),
    "forward1": (20, 46, 50, 51, 56, 61, 77),
    "wforward": (27,),
    "forward3": (29, 31, 32, 34, 36, 39, 43),
    "spread2": (33, 40, 42, 44, 45, 59, 63),
    "warrived": (37,),
    "multiply1": (41, 47, 48, 53, 60, 62, 67),
    "forward2": (58, 64, 66, 68, 69, 75, 78),
    "down1": (70, 71, 72, 73, 74, 76, 79),
    "multiply0": (80, 82, 84, 86, 87, 90, 91),
    "merge1": (81, 83, 85, 88, 89, 97, 112),
    "down0": (92, 93, 94, 95, 96, 100, 104),
    "home1": (98, 99, 103, 105, 107, 109, 120),
    "merge0": (101, 102, 106, 108, 110, 111, 115),
    "home0": (113, 114, 116, 117, 118, 119, 122),
    "finish": (121, 123, 124, 125, 126, 127, 128),
}


def flipped(index, mask):
    value = index
    bit = 0
    while mask >> bit:
        if (mask >> bit) & 1:
            size = 1 << bit
            value = value + size * (1 - 2 * lax.rem(lax.div(index, jnp.int32(size)), jnp.int32(2)))
        bit += 1
    return value


def dot(left, right):
    return jnp.dot(left, right, preferred_element_type=F32)


def kernel(
    groups, chunks,
    tok_hbm, ids_hbm, rw_hbm, wg_hbm, wu_hbm, wd_hbm, out,
    tok, ids, rw, wgu, wd, place, place_t, perm, perm_t,
    sent, held, wsent, warr, whold, xs, acc, hidden, wcol,
    part, relay, got, back_s, back,
    ssems, rsems, wsems, lsems,
):
    node = lax.axis_index("node")
    torus = lax.axis_index("torus")
    rows = tok.shape[0]
    subs = groups * SUB
    fold = groups // 2
    sh = fold * SUB
    slots = fold * CAP
    lots = 4 * slots
    side = CHUNK // 2
    unit = min(128, sh)
    experts = wd.shape[0]
    peers = [j for j in range(groups) if not j & 2] + [j for j in range(groups) if j & 2]
    at_x = (flipped(node, 1), torus)
    at_y = (flipped(node, 2), torus)
    at_z = [(node, flipped(torus, j)) for j in range(groups)]

    barrier = pltpu.get_barrier_semaphore()
    for peer in at_z[1:] + [at_x, at_y]:
        pl.semaphore_signal(barrier, inc=1, device_id=peer, device_id_type=MESH)

    def load(src, dst, at):
        pltpu.make_async_copy(src, dst, lsems.at[at]).start()

    def loaded(ref, at):
        pltpu.make_async_copy(ref, ref, lsems.at[at]).wait()

    load(ids_hbm, ids, 0)
    load(rw_hbm, rw, 1)
    spans = [pl.ds(k * CHUNK, CHUNK) for k in range(chunks)]
    for cols in spans:
        load(tok_hbm.at[:, cols], tok.at[:, cols], 2)
    for cols in spans:
        load(wg_hbm.at[:, cols, :], wgu.at[0, :, cols, :], 3)
        load(wu_hbm.at[:, cols, :], wgu.at[1, :, cols, :], 3)
    for cols in spans:
        load(wd_hbm.at[:, :, cols], wd.at[:, :, cols], 4)

    pr = lax.broadcasted_iota(jnp.int32, (128, 128), 0)
    pc = lax.broadcasted_iota(jnp.int32, (128, 128), 1)
    ur = 128 // PARTS
    perm[...] = (pc == (pr % ur) * PARTS + pr // ur).astype(F32).astype(BF16)
    tr = lax.broadcasted_iota(jnp.int32, (unit, unit), 0)
    tc = lax.broadcasted_iota(jnp.int32, (unit, unit), 1)
    tu = unit // PARTS
    perm_t[...] = (tr == (tc % tu) * PARTS + tc // tu).astype(F32).astype(BF16)

    def distance(at):
        inner = at % fold
        return (inner // 2) * 4 + (at // fold) * 2 + inner % 2

    loaded(ids, 0)
    loaded(rw, 1)
    row = lax.broadcasted_iota(jnp.int32, (subs, rows), 0)
    gid = jnp.bitwise_xor(distance(row // SUB), jnp.full((subs, rows), torus, jnp.int32))
    slot_of = (row // PARTS) % CAP
    part_of = row % PARTS
    hit = jnp.zeros((subs, rows), F32)
    chosen = [jnp.zeros((subs, rows), F32) for _ in range(experts)]
    weights = rw[...].astype(F32)
    for k in range(ids.shape[0]):
        named = jnp.broadcast_to(ids[k : k + 1, :], (subs, rows))
        weight = jnp.broadcast_to(weights[k : k + 1, :], (subs, rows))
        for e in range(experts):
            same = named == gid * experts + e
            hit = jnp.where(same, 1.0, hit)
            chosen[e] = jnp.where(same, weight, chosen[e])
    lower = lax.broadcasted_iota(jnp.int32, (rows, rows), 0) < lax.broadcasted_iota(
        jnp.int32, (rows, rows), 1
    )
    before = dot(hit.astype(BF16), lower.astype(F32).astype(BF16))
    onehot = jnp.where(before == slot_of.astype(F32), hit, 0.0)
    for q in range(PARTS):
        place[q] = jnp.where(part_of == q, onehot, 0.0).astype(BF16)
    lane = lax.broadcasted_iota(jnp.int32, (subs, 128), 1)
    from_j = distance(lax.broadcasted_iota(jnp.int32, (subs, 128), 0) // SUB)
    wrow = jnp.zeros((subs, 128), F32)
    for e in range(experts):
        total = jnp.sum(onehot * chosen[e], axis=1, keepdims=True)
        wrow = jnp.where(lane == from_j * experts + e, total, wrow)
    wsent[...] = wrow.astype(BF16)
    warr[0:SUB] = wrow[0:SUB].astype(BF16)

    def build(k):
        picked = jnp.zeros((subs, WIDE), F32)
        for q in range(PARTS):
            picked += dot(place[q], tok[:, k * CHUNK + q * WIDE : k * CHUNK + (q + 1) * WIDE])
        for b in range(WIDE // QBLOCK):
            block = picked[:, b * QBLOCK : (b + 1) * QBLOCK]
            largest = jnp.max(jnp.abs(block), axis=1, keepdims=True)
            scale = ((largest + 1e-06) * (1.0 / 448.0)).astype(BF16).astype(F32)
            coded = (block / scale).astype(BF16).astype(F32)
            value = (coded * scale).astype(BF16)
            at = k * WIDE + b * QBLOCK
            sent[:, at : at + QBLOCK] = value
            held[0:SUB, at : at + QBLOCK] = value[0:SUB]

    loaded(tok, 2)
    for k in range(EARLY):
        build(k)

    pl.semaphore_wait(barrier, groups + 1)

    def copy(src, dst, send, recv, peer):
        pltpu.make_async_remote_copy(
            src_ref=src, dst_ref=dst, send_sem=send, recv_sem=recv,
            device_id=peer, device_id_type=MESH,
        ).start()

    def remote(kind, k, src, dst, peer):
        late = 1 if kind[0] in "rg" or kind == "zr" else 0
        copy(src, dst, ssems.at[late], rsems.at[KINDS.index(kind), k], peer)

    def wait(kind, k, ref):
        pltpu.make_async_copy(ref, ref, rsems.at[KINDS.index(kind), k]).wait()

    def settle(ref, sem):
        pltpu.make_async_copy(ref, ref, sem).wait()

    def lanes(k):
        return pl.ds(k * WIDE, WIDE)

    classes = ((0, 0, 1), (0, 1, 2), (0, 2, fold), (1, 0, fold))

    def some(count, k):
        return held.at[pl.ds(0, count), lanes(k)]

    def rows_of(c, r, k, lo=None, hi=None):
        h, first, last = classes[c]
        lo = first if lo is None else lo
        hi = last if hi is None else hi
        return held.at[pl.ds((h * 4 + r) * sh + lo * SUB, (hi - lo) * SUB), lanes(k)]

    def exchange(c, k):
        h, lo, hi = classes[c]
        for p in range(lo, hi):
            src = sent.at[pl.ds((h * fold + p) * SUB, SUB), lanes(k)]
            dst = held.at[pl.ds(h * 4 * sh + p * SUB, SUB), lanes(k)]
            remote(f"z{c}", k, src, dst, at_z[peers[h * fold + p]])

    def spread(c, k):
        if c:
            wait(f"z{c}", k, rows_of(c, 0, k))
        by_x = "a0" if c == 1 else f"t{c}"
        by_y = "a0" if c == 0 else f"t{c}"
        remote(by_x, k, rows_of(c, 0, k), rows_of(c, 1, k), at_x)
        remote(by_y, k, rows_of(c, 0, k), rows_of(c, 2, k), at_y)

    def forward(c, k):
        h, lo, hi = classes[c]
        wait(f"t{c}", k, some((hi - lo) * SUB * (1 if c < 2 else 2), k))
        mid = {0: hi, 1: lo}.get(c, (lo + hi) // 2)
        if mid > lo:
            remote(f"a{h}", k, rows_of(c, 1, k, lo, mid), rows_of(c, 3, k, lo, mid), at_y)
        if hi > mid:
            remote(f"a{h}", k, rows_of(c, 2, k, mid, hi), rows_of(c, 3, k, mid, hi), at_x)

    def make(k):
        if k >= EARLY:
            build(k)
        exchange(3, k)
        exchange(1, k)
        spread(0, k)
        if k == 0:
            for p in range(1, groups):
                at = pl.ds(p * SUB, SUB)
                copy(wsent.at[at], warr.at[at], ssems.at[2], wsems.at[0], at_z[peers[p]])

    def wspread(_):
        settle(warr.at[pl.ds(SUB, subs - SUB)], wsems.at[0])
        total = jnp.zeros((SUB, 128), F32)
        for p in range(groups):
            total += warr[p * SUB : (p + 1) * SUB].astype(F32)
        whold[0:SUB] = total.astype(BF16)
        own = whold.at[pl.ds(0, SUB)]
        copy(own, whold.at[pl.ds(SUB, SUB)], ssems.at[3], wsems.at[1], at_x)
        copy(own, whold.at[pl.ds(2 * SUB, SUB)], ssems.at[3], wsems.at[2], at_y)

    def wforward(_):
        near = whold.at[pl.ds(SUB, SUB)]
        settle(near, wsems.at[1])
        copy(near, whold.at[pl.ds(3 * SUB, SUB)], ssems.at[3], wsems.at[2], at_y)

    def warrived(_):
        settle(whold.at[pl.ds(2 * SUB, 2 * SUB)], wsems.at[2])
        er = lax.broadcasted_iota(jnp.int32, (lots, 4 * SUB), 0)
        ec = lax.broadcasted_iota(jnp.int32, (lots, 4 * SUB), 1)
        pick = ec == (er // slots) * SUB + (er % CAP) * PARTS
        spun = dot(pick.astype(F32).astype(BF16), whold[...])
        wl = lax.broadcasted_iota(jnp.int32, (lots, 128), 1)
        place_in = (lax.broadcasted_iota(jnp.int32, (lots, 128), 0) % slots) // CAP
        for h in range(2):
            far = distance(place_in + h * fold)
            for e in range(experts):
                mine = jnp.where(wl == far * experts + e, spun, 0.0)
                column = jnp.sum(mine, axis=1, keepdims=True)
                wcol[h, e] = jnp.broadcast_to(column, (lots, 128))

    def multiply(h, k):
        if h:
            wait("a1", k, some(sh, k))
        else:
            wait("a0", k, some(sh + 2 * SUB, k))
        for u in range(4 * sh // 128):
            at = h * 4 * sh + u * 128
            moved = dot(perm[...], held[at : at + 128, k * WIDE : (k + 1) * WIDE]).astype(BF16)
            for q in range(PARTS):
                xs[h, u * ur : (u + 1) * ur, q * WIDE : (q + 1) * WIDE] = moved[q * ur : (q + 1) * ur]
        if h and k == 0:
            loaded(wgu, 3)
        cols = pl.ds(k * CHUNK, CHUNK)
        for e in range(experts):
            for s in range(2):
                term = dot(xs[h], wgu[s, e, cols, :])
                if k == 0:
                    acc[h, e, s] = term
                else:
                    acc[h, e, s] += term
        if k == chunks - 1:
            for e in range(experts):
                gate = acc[h, e, 0]
                hidden[h, e] = (gate / (1.0 + jnp.exp(-gate)) * acc[h, e, 1]).astype(BF16)

    def down(h, k):
        if h and k == 0:
            loaded(wd, 4)
        total = jnp.zeros((lots, CHUNK), F32)
        for e in range(experts):
            term = dot(hidden[h, e], wd[e, :, k * CHUNK : (k + 1) * CHUNK])
            total += jnp.tile(wcol[h, e], (1, CHUNK // 128)) * term
        part[h, :, spans[k]] = total.astype(BF16)
        here = pl.ds(k * side, side)
        for s, peer in enumerate((at_y, at_x)):
            src = part.at[h, pl.ds(3 * slots, slots), pl.ds(k * CHUNK + s * side, side)]
            remote(f"r{h}", k, src, relay.at[h, s, :, here], peer)

    def merge(h, k):
        here = pl.ds(k * side, side)
        wait(f"r{h}", k, relay.at[h, :, :, here])
        for s, peer in enumerate((at_x, at_y)):
            at, where = pl.ds((s + 1) * slots, slots), pl.ds(k * CHUNK + s * side, side)
            total = part[h, at, where].astype(F32) + relay[h, s, :, here].astype(F32)
            part[h, at, where] = total.astype(BF16)
            remote(f"g{h}", k, part.at[h, at, spans[k]], got.at[h, s, :, spans[k]], peer)

    def home(h, k):
        cols = spans[k]
        wait(f"g{h}", k, got.at[h, :, :, cols])
        total = (
            part[h, 0:slots, cols].astype(F32) + got[h, 0, :, cols].astype(F32) + got[h, 1, :, cols].astype(F32)
        ).astype(BF16)
        for u in range(sh // unit):
            stacked = jnp.concatenate(
                [total[u * tu : (u + 1) * tu, q * WIDE : (q + 1) * WIDE] for q in range(PARTS)], axis=0
            )
            moved = dot(perm_t[...], stacked).astype(BF16)
            at = h * sh + u * unit
            back_s[at : at + unit, k * WIDE : (k + 1) * WIDE] = moved
            if h == 0 and u == 0:
                back[0:SUB, k * WIDE : (k + 1) * WIDE] = moved[0:SUB]
        for p in range(h * fold, (h + 1) * fold):
            if p:
                at = pl.ds(p * SUB, SUB)
                remote("zr", k, back_s.at[at, lanes(k)], back.at[at, lanes(k)], at_z[peers[p]])

    def finish(k):
        if k == 0:
            for q in range(PARTS):
                place_t[q] = place[q].astype(F32).T.astype(BF16)
        wait("zr", k, back.at[pl.ds(SUB, subs - SUB), lanes(k)])
        for q in range(PARTS):
            at = k * CHUNK + q * WIDE
            out[:, at : at + WIDE] = dot(place_t[q], back[:, k * WIDE : (k + 1) * WIDE]).astype(BF16)

    stages = {"make": make, "late": lambda k: exchange(2, k), "finish": finish}
    for c in range(4):
        stages[f"spread{c}"] = functools.partial(spread, c)
        stages[f"forward{c}"] = functools.partial(forward, c)
    for h in range(2):
        for name, stage in (("multiply", multiply), ("down", down), ("merge", merge), ("home", home)):
            stages[f"{name}{h}"] = functools.partial(stage, h)
    once = {"wspread": wspread, "wforward": wforward, "warrived": warrived}
    tasks = [(at, name, k) for name, places in PLACES.items() for k, at in enumerate(places)]
    for _, name, k in sorted(tasks):
        (once.get(name) or stages[name])(k)

    for late in range(2):
        settle(held.at[pl.ds(SUB, 8 * sh - SUB)], ssems.at[late])
    settle(wsent.at[pl.ds(SUB, subs - SUB)], ssems.at[2])
    settle(whold.at[pl.ds(SUB, 3 * SUB)], ssems.at[3])


def shards(tokens, expert_ids, route_weight, w_gate, w_up, w_down):
    groups = lax.axis_size("torus")
    rows, width = tokens.shape
    experts, _, units = w_gate.shape
    chunks = width // CHUNK
    subs = groups * SUB
    fold = groups // 2
    sh = fold * SUB
    slots = fold * CAP
    lots = 4 * slots
    span = chunks * WIDE
    anywhere = pl.BlockSpec(memory_space=pl.ANY)
    args = (tokens, expert_ids.T, route_weight.T, w_gate, w_up, w_down)
    V = pltpu.VMEM
    return pl.pallas_call(
        functools.partial(kernel, groups, chunks),
        out_shape=pltpu.VMEM((rows, width), BF16),
        in_specs=[anywhere] * 6,
        out_specs=pl.BlockSpec(memory_space=pltpu.VMEM),
        scratch_shapes=[
            V((rows, width), BF16),
            V((expert_ids.shape[1], rows), jnp.int32),
            V((expert_ids.shape[1], rows), BF16),
            V((2,) + w_gate.shape, BF16),
            V(w_down.shape, BF16),
            V((PARTS, subs, rows), BF16),
            V((PARTS, rows, subs), BF16),
            V((128, 128), BF16),
            V((min(128, sh), min(128, sh)), BF16),
            V((subs, span), BF16),
            V((8 * sh, span), BF16),
            V((subs, 128), BF16),
            V((subs, 128), BF16),
            V((4 * SUB, 128), BF16),
            V((2, lots, CHUNK), BF16),
            V((2, experts, 2, lots, units), F32),
            V((2, experts, lots, units), BF16),
            V((2, experts, lots, 128), F32),
            V((2, lots, width), BF16),
            V((2, 2, slots, width // 2), BF16),
            V((2, 2, slots, width), BF16),
            V((subs, span), BF16),
            V((subs, span), BF16),
            pltpu.SemaphoreType.DMA((4,)),
            pltpu.SemaphoreType.DMA((len(KINDS), chunks)),
            pltpu.SemaphoreType.DMA((3,)),
            pltpu.SemaphoreType.DMA((5,)),
        ],
        compiler_params=pltpu.CompilerParams(
            collective_id=0, has_side_effects=True, vmem_limit_bytes=60000000
        ),
    )(*[pltpu.with_memory_space_constraint(a, pltpu.HBM) for a in args])


def solution(mesh):
    placed = (
        P(("node", "torus"), None),
        P(("node", "torus"), None),
        P(("node", "torus"), None),
        P("torus", None, "node"),
        P("torus", None, "node"),
        P("torus", "node", None),
    )
    return jax.shard_map(
        shards, mesh=mesh, in_specs=placed, out_specs=P(("node", "torus"), None), check_vma=False
    )
```

time: 56 us -> 45.8 us (0.82)
  Pallas kernels: 53 us -> 44.4 us
  local copies, waits for them, and re-layouts: 2.85 us -> 1.23 us
    pallas_call x1, Pallas kernels: 53 us -> 44.4 us  [shards(): pl.pallas_call(functools.partial(kernel, groups, chunks), out_shape=pltpu...]
    unnamed x1, local copies, waits for them, and re-layouts: 2.85 us -> 1.23 us
where the time goes in v2:
time: 45.8 us; the launch traced here: 45.7 us
  Pallas kernels  44.4 us (97%)
  local copies, waits for them, and re-layouts  1.23 us (3%)
    pallas_call x1, Pallas kernels, shards(): pl.pallas_call(functools.partial(kernel, groups, chunks), out_shape=pltpu...  44.4 us
    unnamed x1, local copies, waits for them, and re-layouts  1.23 us

profile of v2, /device:TPU:0, one launch (start us, length us, event | category | flops | bytes accessed | tf_op | source)
XLA Modules:
  0.0 45.7 jit_solution(17735430712190754527)
XLA Ops:
  0.0 44.4 %shard_map.64 = bf16[128,7168]{1,0:T(8,128)(2,1)S(1)} custom-call(bf16[128,7168]{1,0:T(8,128)(2,1)} %tok_hbm.1, s32[8,128]{1,0:T(8,128)} %bitcast.2, bf16[8,128]{1,0:T(8,128)(2,1)} %bitcast.3, bf16[2,7168,256]{2,1,0:T(8,128)(2,1)} %wg_hbm.1, bf16[2,7168,256]{2,1,0:T(8,128)(2,1)} %wu_hbm.1, bf16[2,256,7168]{2,1,0:T(8,128)(2,1)} %wd_hbm.1), custom_call_target="tpu_custom_call" | custom-call | tf_op jit(solution)/shard_map/pallas_call | solution.py:376
  44.4 1.2 %copy.8 = bf16[128,7168]{1,0:T(8,128)(2,1)} copy(bf16[128,7168]{1,0:T(8,128)(2,1)S(1)} %shard_map.64) | data formatting | bytes 3670016
